TPU v7x, 32 devices: a whole 2x2x4 slice. The times are simulated.
32 devices in a mesh: dom: 32 (over z, y, x, core).
Axes of the slice: x: 2, y: 2, z: 4, core: 2. Of those that a mesh axis runs over, the one named last changes fastest.
Arguments:
- wing_jitter: float32 [3, 262144], P(None, 'dom'), may hold values from 0 to 1
- live_blocks: int32 [32], P('dom'), may hold values from 1 to 64, as said below
- smoothing: float32 [262144], P('dom'), may hold values from 0.3 to 3
- displacement: float32 [3, 262144], P(None, 'dom'), may hold values from -20 to 20
- fluid_jitter: float32 [3, 98304], P(None, 'dom'), may hold values from 0 to 1
Outputs:
- coefs: float32 [3, 262144], P(None, 'dom')
- residual: float32 [3, 262144], P(None, 'dom')
- fluid_values: float32 [3, 98304], P(None, 'dom')
Inputs may be any that keep to these rules, and one draw needn't show every extreme that they name: `live_blocks`: some device holds 64 live blocks, and some device other than the first and the last holds 1.
All inputs are finite; a program needn't handle non-finite values.
Results may differ from a plain program's by a relative error of at most 0.0003.
Values sent between devices are 32-bit elements; how exact they have to be, the bound alone decides.
A program may use at most 64 MiB of HBM per device.

v0:
```python
import jax
import jax.numpy as jnp
from jax import lax
from jax.sharding import PartitionSpec as P

BLK = 128
ITERS = 3


stretch_factors = (1.0, 6.0, 6.0)


def from_behind(block, axis, distance):
    devices = range(lax.axis_size(axis))
    route = [(i - distance, i) for i in devices if i - distance in devices]
    return lax.ppermute(block, axis, route)


def wendland(row_points, col_points):
    spread = (row_points[0][:, None] - col_points[0][None, :]) ** 2
    spread = spread + (row_points[1][:, None] - col_points[1][None, :]) ** 2
    spread = spread + (row_points[2][:, None] - col_points[2][None, :]) ** 2
    scaled = jnp.sqrt(spread) * 0.5
    remain = jnp.maximum(1.0 - scaled, 0.0)
    return remain * remain * remain * remain * (4.0 * scaled + 1.0)


def block_ends(blocks, live_count):
    tail_index = live_count - 2 + jnp.arange(2, dtype=jnp.int32)
    tail_flags = (tail_index >= 0).astype(jnp.float32)
    tail_blocks = jnp.take(blocks, jnp.maximum(tail_index, 0), axis=1)
    head_flags = (jnp.arange(2, dtype=jnp.int32) < live_count).astype(jnp.float32)
    head_blocks = blocks[:, :2]
    return (tail_blocks, tail_flags, head_blocks, head_flags)


def join_left(nearer, farther, pick):
    return jnp.stack([jnp.where(pick, nearer[:, 0], farther[:, 1]), nearer[:, 1]], axis=1)


def join_right(nearer, farther, pick):
    return jnp.stack([nearer[:, 0], jnp.where(pick, nearer[:, 1], farther[:, 0])], axis=1)


def extend(own_blocks, left_pair, right_pair, live_count):
    padded = jnp.concatenate([left_pair, own_blocks, jnp.zeros_like(left_pair)], axis=1)
    return lax.dynamic_update_slice_in_dim(padded, right_pair, live_count + 2, axis=1)


def two_products(residual, precond, image):
    return lax.psum((jnp.sum(residual * precond, axis=1), jnp.sum(precond * image, axis=1)), "dom")


def per_device(wing_jitter, live_blocks, smoothing, displacement, fluid_jitter):
    block_count = wing_jitter.shape[1] // BLK
    fluid_count = fluid_jitter.shape[1] // BLK
    live_count = live_blocks[0]
    factors = jnp.array(stretch_factors, jnp.float32)[:, None, None]
    own_points = wing_jitter.reshape(3, block_count, BLK) * factors
    own_flags = (jnp.arange(block_count, dtype=jnp.int32) < live_count).astype(jnp.float32)
    ends_of = {}
    neighbour_counts = {}
    for offset in (1, 2, -1, -2):
        points, counts = from_behind((own_points, live_blocks), "dom", offset)
        tail_blocks, tail_flags, head_blocks, head_flags = block_ends(points, counts[0])
        neighbour_counts[offset] = counts[0]
        ends_of[offset] = (tail_blocks, tail_flags) if offset > 0 else (head_blocks, head_flags)
    left_pick = ends_of[1][1][0] > 0
    right_pick = ends_of[-1][1][1] > 0
    left_points = join_left(ends_of[1][0], ends_of[2][0], left_pick)
    right_points = join_right(ends_of[-1][0], ends_of[-2][0], right_pick)
    left_flags = join_left(ends_of[1][1][None, :, None], ends_of[2][1][None, :, None], left_pick)
    right_flags = join_right(
        ends_of[-1][1][None, :, None], ends_of[-2][1][None, :, None], right_pick
    )
    ext_points = extend(own_points, left_points, right_points, live_count)
    ext_flags = extend(own_flags[None, :, None], left_flags, right_flags, live_count)
    ext_along = jnp.arange(block_count + 4, dtype=jnp.float32) - 2.0
    ext_points = ext_points.at[0].add(ext_along[:, None]).reshape(3, -1)
    col_flags = jnp.broadcast_to(ext_flags[0], (block_count + 4, BLK)).reshape(-1)
    row_points = (
        own_points.at[0].add(jnp.arange(block_count, dtype=jnp.float32)[:, None]).reshape(3, -1)
    )
    row_mask = jnp.repeat(own_flags, BLK)
    diagonal = 1.0 + smoothing

    def value_context(blocks):
        pieces = {}
        for offset in (1, 2, -1, -2):
            moved = from_behind(blocks, "dom", offset)
            tail_part, tail_marks, head_part, head_marks = block_ends(
                moved, neighbour_counts[offset]
            )
            pieces[offset] = tail_part if offset > 0 else head_part
        left_values = join_left(pieces[1], pieces[2], left_pick)
        right_values = join_right(pieces[-1], pieces[-2], right_pick)
        return extend(blocks, left_values, right_values, live_count).reshape(3, -1)

    def apply(vector):
        ext_values = value_context(vector.reshape(3, block_count, BLK))

        def row_group(group):
            first_row = group * (2 * BLK)
            points = lax.dynamic_slice_in_dim(row_points, first_row, 2 * BLK, 1)
            col_points = lax.dynamic_slice_in_dim(ext_points, first_row, 6 * BLK, 1)
            flags = lax.dynamic_slice_in_dim(col_flags, first_row, 6 * BLK, 0)
            kernel = wendland(points, col_points) * flags[None, :]
            col_values = lax.dynamic_slice_in_dim(ext_values, first_row, 6 * BLK, 1)
            return jnp.einsum("cj,ij->ci", col_values, kernel, precision=lax.Precision.HIGHEST)

        result = lax.map(row_group, jnp.arange(block_count // 2, dtype=jnp.int32))
        result = result.transpose(1, 0, 2).reshape(3, -1)
        return result * row_mask + smoothing * vector

    rhs = displacement * row_mask
    coefs = jnp.zeros_like(rhs)
    residual = rhs
    precond = residual / diagonal
    image = apply(precond)
    norm_now, product = two_products(residual, precond, image)
    step_size = norm_now / product
    direction, along = (precond, image)
    for iteration in range(ITERS):
        coefs = coefs + step_size[:, None] * direction
        residual = residual - step_size[:, None] * along
        if iteration + 1 < ITERS:
            precond = residual / diagonal
            image = apply(precond)
            norm_next, product = two_products(residual, precond, image)
            momentum = norm_next / norm_now
            step_size = norm_next / (product - momentum * norm_next / step_size)
            direction = precond + momentum[:, None] * direction
            along = image + momentum[:, None] * along
            norm_now = norm_next
    anchors = jnp.arange(fluid_count, dtype=jnp.int32) * live_count // fluid_count
    fluid_points = fluid_jitter.reshape(3, fluid_count, BLK) * factors
    fluid_points = fluid_points.at[0].add(anchors.astype(jnp.float32)[:, None])
    coef_ext = value_context(coefs.reshape(3, block_count, BLK))

    def fluid_block(index):
        start_col = anchors[index] * BLK
        points = lax.dynamic_index_in_dim(fluid_points, index, 1, keepdims=False)
        col_points = lax.dynamic_slice_in_dim(ext_points, start_col, 5 * BLK, 1)
        flags = lax.dynamic_slice_in_dim(col_flags, start_col, 5 * BLK, 0)
        kernel = wendland(points, col_points) * flags[None, :]
        col_values = lax.dynamic_slice_in_dim(coef_ext, start_col, 5 * BLK, 1)
        return jnp.einsum("cj,ij->ci", col_values, kernel, precision=lax.Precision.HIGHEST)

    fluid_values = lax.map(fluid_block, jnp.arange(fluid_count, dtype=jnp.int32))
    fluid_values = fluid_values.transpose(1, 0, 2).reshape(3, -1)
    return (coefs, residual, fluid_values)


def solution(mesh):
    return jax.shard_map(
        per_device,
        mesh=mesh,
        in_specs=(P(None, "dom"), P("dom"), P("dom"), P(None, "dom"), P(None, "dom")),
        out_specs=(P(None, "dom"), P(None, "dom"), P(None, "dom")),
        check_vma=False,
    )
```

profile of v0, /device:TPU:0, one launch (start us, length us, event | category | flops | bytes accessed | tf_op | source)
XLA Modules:
  0.0 640.1 jit_solution(5302028449259898660)
XLA Ops:
  0.6 3.0 collective-permute-start
  5.4 3.9 collective-permute-start.1
  9.3 3.4 collective-permute-start.2
  12.7 4.0 collective-permute-start.3
  16.8 1.4 collective-permute-start.7
  18.4 3.4 collective-permute-start.8
  24.5 2.0 collective-permute-done.5
  44.5 1.4 scatter-add.11
  46.1 5.8 collective-permute-done.6
  51.9 91.1 %while.51 = (s32[]{:T(128)}, f32[32,3,256]{2,1,0:T(4,128)S(1)}, s32[32]{0:T(128)S(1)}, f32[3,8704]{1,0:T(4,128)S(1)}, f32[3,8192]{1,0:T(4,128)S(1)}, /*index=5*/...) while((s32[]{:T(128)}, f32[32,3,256]{2,1,0:T(4,128)S(1)}, ...), condition=%wide.region_3.5_spmd, body=%wide.region_2.4_spmd.sunk | while | flops 10616842 | bytes 66836 | solution.py:111
  56.3 1.3 fusion.174
  59.2 1.3 fusion.174
  67.7 1.3 fusion.174
  70.6 1.3 fusion.174
  79.1 1.3 fusion.174
  82.0 1.3 fusion.174
  90.5 1.3 fusion.174
  93.3 1.3 fusion.174
  101.9 1.3 fusion.174
  104.7 1.3 fusion.174
  113.3 1.3 fusion.174
  116.1 1.3 fusion.174
  121.8 1.3 fusion.174
  124.7 1.3 fusion.174
  127.5 1.3 fusion.174
  133.2 1.3 fusion.174
  136.0 1.3 fusion.174
  138.9 1.3 fusion.174
  141.7 1.3 fusion.174
  143.3 47.0 %all-reduce.2 = (f32[3]{0:T(128)S(1)}, f32[3]{0:T(128)S(1)}) all-reduce(f32[3]{0:T(128)S(1)} %get-tuple-element.425, f32[3]{0:T(128)S(1)} %get-tuple-element.424), channel_id=1, replica_groups=mesh['dom'=32] {'dom'}, use_global_device_ids=true, to_apply=%region_1.2 | all-reduce | flops 6 | bytes 48 | tf_op jit(solution)/shard_map/psum | solution.py:51
  190.5 4.2 collective-permute-start.13
  197.3 3.0 collective-permute-start.12
  202.1 2.1 collective-permute-done.15
  204.3 94.4 %while.52 = (s32[]{:T(128)}, f32[32,3,256]{2,1,0:T(4,128)S(1)}, s32[32]{0:T(128)S(1)}, f32[3,8704]{1,0:T(4,128)S(1)}, f32[3,8192]{1,0:T(4,128)S(1)}, /*index=5*/...) while((s32[]{:T(128)}, f32[32,3,256]{2,1,0:T(4,128)S(1)}, ...), condition=%wide.region_9.11_spmd, body=%wide.region_8.10_spmd.sunk | while | flops 10616842 | bytes 66836 | solution.py:111
  214.8 1.3 fusion.177
  235.5 1.3 fusion.177
  250.2 1.3 fusion.177
  294.5 1.3 fusion.177
  299.0 43.5 %all-reduce.1 = (f32[3]{0:T(128)S(1)}, f32[3]{0:T(128)S(1)}) all-reduce(f32[3]{0:T(128)S(1)} %get-tuple-element.427, f32[3]{0:T(128)S(1)} %get-tuple-element.426), channel_id=1, replica_groups=mesh['dom'=32] {'dom'}, use_global_device_ids=true, to_apply=%region_7.9 | all-reduce | flops 6 | bytes 48 | tf_op jit(solution)/shard_map/psum | solution.py:51
  342.7 4.2 collective-permute-start.17
  349.5 3.0 collective-permute-start.16
  354.3 2.1 collective-permute-done.19
  356.5 91.1 %while.53 = (s32[]{:T(128)}, f32[32,3,256]{2,1,0:T(4,128)S(1)}, s32[32]{0:T(128)S(1)}, f32[3,8704]{1,0:T(4,128)S(1)}, f32[3,8192]{1,0:T(4,128)S(1)}, /*index=5*/...) while((s32[]{:T(128)}, f32[32,3,256]{2,1,0:T(4,128)S(1)}, ...), condition=%wide.region_15.17_spmd, body=%wide.region_14.16_spmd.sunk | while | flops 10616842 | bytes 66836 | solution.py:111
  447.8 43.5 %all-reduce = (f32[3]{0:T(128)S(1)}, f32[3]{0:T(128)S(1)}) all-reduce(f32[3]{0:T(128)S(1)} %get-tuple-element.429, f32[3]{0:T(128)S(1)} %get-tuple-element.428), channel_id=1, replica_groups=mesh['dom'=32] {'dom'}, use_global_device_ids=true, to_apply=%region_13.15 | all-reduce | flops 6 | bytes 48 | tf_op jit(solution)/shard_map/psum | solution.py:51
  492.2 4.2 collective-permute-start.21
  499.0 3.0 collective-permute-start.20
  503.9 2.1 collective-permute-done.23
  506.0 134.1 %while.54 = (s32[]{:T(128)}, f32[24,3,128]{2,1,0:T(4,128)}, s32[24]{0:T(128)S(1)}, s32[24]{0:T(128)S(1)}, f32[3,8704]{1,0:T(4,128)S(1)}, /*index=5*/f32[3,24,128...) while((s32[]{:T(128)}, f32[24,3,128]{2,1,0:T(4,128)}, ...), condition=%wide.region_19.21_spmd, body=%wide.region_18.20_spmd.sunk | while | flops 4423691 | bytes 54573 | solution.py:149
  (732 shorter events, 281.1 us)
Async XLA Ops:
  0.6 3.7 copy-start.1
  0.6 17.7 %collective-permute-start = (s32[1]{0:T(128)}, s32[1]{0:T(128)}, u32[]{:S(2)}, u32[]{:S(2)}) collective-permute-start(s32[1]{0:T(128)} %param.23), channel_id=1, source_target_pairs={{0,1},{1,2},{2,3},{3,4},{4,5},{5,6},{6,7},{7,8},{8,9},{9,10},{10,1... | collective-permute-start | bytes 20 | tf_op jit(solution)/shard_map/ppermute | solution.py:16
  4.4 12.4 %copy-start.3 = (f32[3,8192]{1,0:T(4,128)S(1)}, f32[3,8192]{1,0:T(4,128)}, u32[]{:S(2)}) copy-start(f32[3,8192]{1,0:T(4,128)} %param.22) | copy-start | bytes 294916
  4.4 12.4 %copy-start.5 = (f32[3]{0:T(128)S(1)}, f32[3]{0:T(128)}, u32[]{:S(2)}) copy-start(f32[3]{0:T(128)} %constant.335.clone) | copy-start | bytes 40
  5.4 32.4 %collective-permute-start.1 = (f32[3,64,128]{2,0,1:T(4,128)S(1)}, f32[3,64,128]{2,0,1:T(4,128)S(1)}, u32[]{:S(2)}, u32[]{:S(2)}) collective-permute-start(f32[3,64,128]{2,0,1:T(4,128)S(1)} %fusion.150), channel_id=1, source_target_pairs={{0,1},{1,2},{2,3},{3,4},{4,5},{5,6},{6,7},{7,8},{8,9},{9,10},{10,1... | collective-permute-start | bytes 294920 | tf_op jit(solution)/shard_map/ppermute | solution.py:16
  9.3 32.3 %collective-permute-start.2 = (f32[3,64,128]{2,0,1:T(4,128)S(1)}, f32[3,64,128]{2,0,1:T(4,128)S(1)}, u32[]{:S(2)}, u32[]{:S(2)}) collective-permute-start(f32[3,64,128]{2,0,1:T(4,128)S(1)} %fusion.150), channel_id=1, source_target_pairs={{0,2},{1,3},{2,4},{3,5},{4,6},{5,7},{6,8},{7,9},{8,10},{9,11},{10,... | collective-permute-start | bytes 294920 | tf_op jit(solution)/shard_map/ppermute | solution.py:16
  12.7 9.7 %collective-permute-start.3 = (s32[1]{0:T(128)}, s32[1]{0:T(128)}, u32[]{:S(2)}, u32[]{:S(2)}) collective-permute-start(s32[1]{0:T(128)} %param.23), channel_id=1, source_target_pairs={{0,2},{1,3},{2,4},{3,5},{4,6},{5,7},{6,8},{7,9},{8,10},{9,11},{10,... | collective-permute-start | bytes 20 | tf_op jit(solution)/shard_map/ppermute | solution.py:16
  16.8 22.9 %collective-permute-start.7 = (f32[3,64,128]{2,0,1:T(4,128)S(1)}, f32[3,64,128]{2,0,1:T(4,128)S(1)}, u32[]{:S(2)}, u32[]{:S(2)}) collective-permute-start(f32[3,64,128]{2,0,1:T(4,128)S(1)} %bitcast_multiply_fusion), channel_id=1, source_target_pairs={{0,1},{1,2},{2,3},{3,4},{4,5},{5,6},{6,7},{7,8},{8,9},{9,10},{10,1... | collective-permute-start | bytes 294920 | tf_op jit(solution)/shard_map/ppermute | solution.py:16
  18.4 25.2 %collective-permute-start.8 = (f32[3,64,128]{2,0,1:T(4,128)S(1)}, f32[3,64,128]{2,0,1:T(4,128)S(1)}, u32[]{:S(2)}, u32[]{:S(2)}) collective-permute-start(f32[3,64,128]{2,0,1:T(4,128)S(1)} %bitcast_multiply_fusion), channel_id=1, source_target_pairs={{0,2},{1,3},{2,4},{3,5},{4,6},{5,7},{6,8},{7,9},{8,10},{9,11},{10,... | collective-permute-start | bytes 294920 | tf_op jit(solution)/shard_map/ppermute | solution.py:16
  22.5 4.0 collective-permute-start.5
  26.5 6.5 %collective-permute-start.11 = (s32[1]{0:T(128)}, s32[1]{0:T(128)}, u32[]{:S(2)}, u32[]{:S(2)}) collective-permute-start(s32[1]{0:T(128)} %param.23), channel_id=1, source_target_pairs={{2,0},{3,1},{4,2},{5,3},{6,4},{7,5},{8,6},{9,7},{10,8},{11,9},{12,... | collective-permute-start | bytes 20 | tf_op jit(solution)/shard_map/ppermute | solution.py:16
  32.9 11.4 %collective-permute-start.10 = (f32[3,64,128]{2,0,1:T(4,128)S(1)}, f32[3,64,128]{2,0,1:T(4,128)S(1)}, u32[]{:S(2)}, u32[]{:S(2)}) collective-permute-start(f32[3,64,128]{2,0,1:T(4,128)S(1)} %bitcast_multiply_fusion), channel_id=1, source_target_pairs={{2,0},{3,1},{4,2},{5,3},{6,4},{7,5},{8,6},{9,7},{10,8},{11,9},{12,... | collective-permute-start | bytes 294920 | tf_op jit(solution)/shard_map/ppermute | solution.py:16
  37.8 6.5 %collective-permute-start.9 = (f32[3,64,128]{2,0,1:T(4,128)S(1)}, f32[3,64,128]{2,0,1:T(4,128)S(1)}, u32[]{:S(2)}, u32[]{:S(2)}) collective-permute-start(f32[3,64,128]{2,0,1:T(4,128)S(1)} %bitcast_multiply_fusion), channel_id=1, source_target_pairs={{1,0},{2,1},{3,2},{4,3},{5,4},{6,5},{7,6},{8,7},{9,8},{10,9},{11,1... | collective-permute-start | bytes 294920 | tf_op jit(solution)/shard_map/ppermute | solution.py:16
  39.7 6.4 %collective-permute-start.4 = (f32[3,64,128]{2,0,1:T(4,128)S(1)}, f32[3,64,128]{2,0,1:T(4,128)S(1)}, u32[]{:S(2)}, u32[]{:S(2)}) collective-permute-start(f32[3,64,128]{2,0,1:T(4,128)S(1)} %fusion.150), channel_id=1, source_target_pairs={{1,0},{2,1},{3,2},{4,3},{5,4},{6,5},{7,6},{8,7},{9,8},{10,9},{11,1... | collective-permute-start | bytes 294920 | tf_op jit(solution)/shard_map/ppermute | solution.py:16
  41.6 10.2 %collective-permute-start.6 = (f32[3,64,128]{2,0,1:T(4,128)S(1)}, f32[3,64,128]{2,0,1:T(4,128)S(1)}, u32[]{:S(2)}, u32[]{:S(2)}) collective-permute-start(f32[3,64,128]{2,0,1:T(4,128)S(1)} %fusion.150), channel_id=1, source_target_pairs={{2,0},{3,1},{4,2},{5,3},{6,4},{7,5},{8,6},{9,7},{10,8},{11,9},{12,... | collective-permute-start | bytes 294920 | tf_op jit(solution)/shard_map/ppermute | solution.py:16
  51.9 91.1 %copy-start = (f32[3,8192]{1,0:T(4,128)S(1)}, f32[3,8192]{1,0:T(4,128)}, u32[]{:S(2)}) copy-start(f32[3,8192]{1,0:T(4,128)} %param.25) | copy-start | bytes 294916
  190.3 4.3 copy-start.4
  190.5 9.9 %collective-permute-start.13 = (f32[3,64,128]{2,0,1:T(4,128)S(1)}, f32[3,64,128]{2,0,1:T(4,128)S(1)}, u32[]{:S(2)}, u32[]{:S(2)}) collective-permute-start(f32[3,64,128]{2,0,1:T(4,128)S(1)} %get-tuple-element.501), channel_id=1, source_target_pairs={{0,2},{1,3},{2,4},{3,5},{4,6},{5,7},{6,8},{7,9},{8,10},{9,11},{10,... | collective-permute-start | bytes 294920 | tf_op jit(solution)/shard_map/ppermute | solution.py:16
  194.7 7.4 %collective-permute-start.14 = (f32[3,64,128]{2,0,1:T(4,128)S(1)}, f32[3,64,128]{2,0,1:T(4,128)S(1)}, u32[]{:S(2)}, u32[]{:S(2)}) collective-permute-start(f32[3,64,128]{2,0,1:T(4,128)S(1)} %get-tuple-element.501), channel_id=1, source_target_pairs={{1,0},{2,1},{3,2},{4,3},{5,4},{6,5},{7,6},{8,7},{9,8},{10,9},{11,1... | collective-permute-start | bytes 294920 | tf_op jit(solution)/shard_map/ppermute | solution.py:16
  196.0 8.2 %collective-permute-start.15 = (f32[3,64,128]{2,0,1:T(4,128)S(1)}, f32[3,64,128]{2,0,1:T(4,128)S(1)}, u32[]{:S(2)}, u32[]{:S(2)}) collective-permute-start(f32[3,64,128]{2,0,1:T(4,128)S(1)} %get-tuple-element.501), channel_id=1, source_target_pairs={{2,0},{3,1},{4,2},{5,3},{6,4},{7,5},{8,6},{9,7},{10,8},{11,9},{12,... | collective-permute-start | bytes 294920 | tf_op jit(solution)/shard_map/ppermute | solution.py:16
  197.3 4.0 collective-permute-start.12
  342.7 9.9 %collective-permute-start.17 = (f32[3,64,128]{2,0,1:T(4,128)S(1)}, f32[3,64,128]{2,0,1:T(4,128)S(1)}, u32[]{:S(2)}, u32[]{:S(2)}) collective-permute-start(f32[3,64,128]{2,0,1:T(4,128)S(1)} %bitcast.162), channel_id=1, source_target_pairs={{0,2},{1,3},{2,4},{3,5},{4,6},{5,7},{6,8},{7,9},{8,10},{9,11},{10,... | collective-permute-start | bytes 294920 | tf_op jit(solution)/shard_map/ppermute | solution.py:16
  346.9 7.4 %collective-permute-start.18 = (f32[3,64,128]{2,0,1:T(4,128)S(1)}, f32[3,64,128]{2,0,1:T(4,128)S(1)}, u32[]{:S(2)}, u32[]{:S(2)}) collective-permute-start(f32[3,64,128]{2,0,1:T(4,128)S(1)} %bitcast.163), channel_id=1, source_target_pairs={{1,0},{2,1},{3,2},{4,3},{5,4},{6,5},{7,6},{8,7},{9,8},{10,9},{11,1... | collective-permute-start | bytes 294920 | tf_op jit(solution)/shard_map/ppermute | solution.py:16
  348.2 8.2 %collective-permute-start.19 = (f32[3,64,128]{2,0,1:T(4,128)S(1)}, f32[3,64,128]{2,0,1:T(4,128)S(1)}, u32[]{:S(2)}, u32[]{:S(2)}) collective-permute-start(f32[3,64,128]{2,0,1:T(4,128)S(1)} %bitcast.164), channel_id=1, source_target_pairs={{2,0},{3,1},{4,2},{5,3},{6,4},{7,5},{8,6},{9,7},{10,8},{11,9},{12,... | collective-permute-start | bytes 294920 | tf_op jit(solution)/shard_map/ppermute | solution.py:16
  349.5 4.0 collective-permute-start.16
  492.2 11.7 %copy-start.2 = (f32[3,8192]{1,0:T(4,128)}, f32[3,8192]{1,0:T(4,128)S(1)}, u32[]{:S(2)}) copy-start(f32[3,8192]{1,0:T(4,128)S(1)} %get-tuple-element.516) | copy-start | bytes 294916
  492.2 9.9 %collective-permute-start.21 = (f32[3,64,128]{2,0,1:T(4,128)S(1)}, f32[3,64,128]{2,0,1:T(4,128)S(1)}, u32[]{:S(2)}, u32[]{:S(2)}) collective-permute-start(f32[3,64,128]{2,0,1:T(4,128)S(1)} %bitcast.176), channel_id=1, source_target_pairs={{0,2},{1,3},{2,4},{3,5},{4,6},{5,7},{6,8},{7,9},{8,10},{9,11},{10,... | collective-permute-start | bytes 294920 | tf_op jit(solution)/shard_map/ppermute | solution.py:16
  496.4 7.4 %collective-permute-start.22 = (f32[3,64,128]{2,0,1:T(4,128)S(1)}, f32[3,64,128]{2,0,1:T(4,128)S(1)}, u32[]{:S(2)}, u32[]{:S(2)}) collective-permute-start(f32[3,64,128]{2,0,1:T(4,128)S(1)} %bitcast.177), channel_id=1, source_target_pairs={{1,0},{2,1},{3,2},{4,3},{5,4},{6,5},{7,6},{8,7},{9,8},{10,9},{11,1... | collective-permute-start | bytes 294920 | tf_op jit(solution)/shard_map/ppermute | solution.py:16
  497.7 8.2 %collective-permute-start.23 = (f32[3,64,128]{2,0,1:T(4,128)S(1)}, f32[3,64,128]{2,0,1:T(4,128)S(1)}, u32[]{:S(2)}, u32[]{:S(2)}) collective-permute-start(f32[3,64,128]{2,0,1:T(4,128)S(1)} %bitcast.178), channel_id=1, source_target_pairs={{2,0},{3,1},{4,2},{5,3},{6,4},{7,5},{8,6},{9,7},{10,8},{11,9},{12,... | collective-permute-start | bytes 294920 | tf_op jit(solution)/shard_map/ppermute | solution.py:16
  499.0 4.0 collective-permute-start.20
where the time goes:
time: 646 us; the launch traced here: 640 us
  matrix products  157 us (24%)
  blocking collectives  134 us (21%)
  loops' own time  133 us (21%)
  local copies, waits for them, and re-layouts  131 us (20%)
  starting transfers between devices  56.2 us (9%)
  waiting for transfers between devices  15.1 us (2%)
  other arithmetic  8.18 us (1%)
    psum x3, blocking collectives, two_products(): lax.psum((jnp.sum(residual * precond, axis=1), jnp.sum(precond * image, a...  134 us
    dot_general x96, matrix products, row_group(): jnp.einsum('cj,ij->ci', col_values, kernel, precision=lax.Precision.HIGHEST)  126 us
    another operation x1, loops' own time, per_device(): lax.map(fluid_block, jnp.arange(fluid_count, dtype=jnp.int32))  66.8 us
    another operation x3, loops' own time, apply(): result = lax.map(row_group, jnp.arange(block_count // 2, dtype=jnp.int32))  65.9 us
    dynamic_slice x96, local copies, waits for them, and re-layouts, apply(): result = lax.map(row_group, jnp.arange(block_count // 2, dtype=jnp.int32))  59.9 us
    ppermute x24, starting transfers between devices, from_behind(): return lax.ppermute(block, axis, route)  56.2 us
    dot_general x24, matrix products, fluid_block(): jnp.einsum('cj,ij->ci', col_values, kernel, precision=lax.Precision.HIGHEST)  30.9 us
    slice x216, local copies, waits for them, and re-layouts, wendland(): spread = (row_points[0][:, None] - col_points[0][None, :]) ** 2  20 us
  transfers between devices with their start and end apart: 24, of which 8 were waited for; matrix products, arithmetic and copies ran while one was open for 3% of the time, Pallas kernels for 0%

commit v1 on v0

v1 whole, which is shorter than its diff:
```python
import functools

import jax
import jax.numpy as jnp
from jax import lax
from jax.experimental import pallas as pl
from jax.experimental.pallas import tpu as pltpu
from jax.sharding import PartitionSpec as P

BLK = 128
ITERS = 3
BAND = 5
FAR = 1.0e4
F32 = jnp.float32
BF16 = jnp.bfloat16


def phi_of(row, col):
    dx = row[0] - col[0]
    dy = row[1] - col[1]
    dz = row[2] - col[2]
    spread = jnp.maximum(dx * dx + dy * dy + dz * dz, 1e-30)
    scaled = spread * lax.rsqrt(spread)
    remain = jnp.maximum(1.0 - scaled, 0.0)
    square = remain * remain
    return square * square * (5.0 - 4.0 * remain)


def build(dest, columns, first_col, row):
    for delta in range(BAND):
        at = pl.multiple_of(first_col + delta * BLK, BLK)
        cols = columns[pl.ds(at, BLK), :]
        value = phi_of([cols[:, c:c + 1] for c in range(3)], row)
        high = value.astype(BF16)
        low = (value - high.astype(F32)).astype(BF16)
        dest[delta * BLK:(delta + 1) * BLK, 0:BLK] = high
        dest[delta * BLK:(delta + 1) * BLK, BLK:] = low


def split(v):
    high = v.astype(BF16).astype(F32)
    return jnp.concatenate([high, v - high], axis=0).astype(BF16)


def solver(n_dev, nb, live_ref, wing_ref, smooth_ref, disp_ref,
           coef_out, resid_out, points, coef_ext,
           kmat, columns, ends, halo, sums, vext, zbuf, rbuf, dbuf, abuf, cbuf, ibuf, wbuf,
           inv, halo_send, halo_recv, sum_send, sum_recv):
    me = lax.axis_index("dom")
    count = live_ref[0]
    width = nb * BLK
    halo[...] = jnp.zeros_like(halo)
    barrier = pltpu.get_barrier_semaphore()

    def greet(k, carry):
        pl.semaphore_signal(barrier, inc=1, device_id=(lax.rem(me + k, n_dev),),
                            device_id_type=pl.DeviceIdType.MESH)
        return carry

    lax.fori_loop(1, n_dev, greet, 0)

    block_of = lax.broadcasted_iota(jnp.int32, (8, width), 1) >> 7
    live = block_of < count
    along_x = block_of.astype(F32)
    row_id = lax.broadcasted_iota(jnp.int32, (8, width), 0)
    zbuf[...] = jnp.zeros_like(zbuf)
    zbuf[0:3, :] = wing_ref[...]
    scale = jnp.where(row_id == 0, 0.5, 3.0)
    pts = zbuf[...] * scale + jnp.where(row_id == 0, along_x * 0.5, 0.0)
    pts = jnp.where(live, pts, FAR)
    points[:, 2 * BLK:2 * BLK + width] = pts
    smooth = jnp.broadcast_to(smooth_ref[...], (8, width))
    inv[...] = 1.0 / (1.0 + smooth)
    rbuf[...] = jnp.zeros_like(rbuf)
    rbuf[0:3, :] = disp_ref[...]
    rbuf[...] = jnp.where(live, rbuf[...], 0.0)
    zbuf[...] = rbuf[...] * inv[...]

    row8 = lax.broadcasted_iota(jnp.int32, (8, BLK), 0)
    lane8 = lax.broadcasted_iota(jnp.int32, (8, BLK), 1)

    def picked(ref, start, which):
        total = jnp.zeros((8, BLK), F32)
        for b in range(nb):
            total = total + jnp.where(which == b, ref[:, start + b * BLK:start + (b + 1) * BLK], 0.0)
        return total

    two = (count >= 2).astype(F32)

    def shifted(p, base):
        return jnp.where(row8 == 0, p - base * 0.5, p)

    def pack(p, z, flag):
        low = jnp.concatenate([p[0:3, :], z[0:3, :], jnp.full((2, BLK), 1.0, F32) * flag], axis=0)
        return low

    countf = count.astype(F32)
    own = 2 * BLK
    ends[0, 0, :, 0:BLK] = pack(shifted(picked(points, own, count - 2), countf), picked(zbuf, 0, count - 2), two)
    ends[0, 0, :, BLK:] = pack(shifted(picked(points, own, count - 1), countf), picked(zbuf, 0, count - 1), 1.0)
    ends[0, 1, :, 0:BLK] = pack(points[:, own:own + BLK], zbuf[:, 0:BLK], 1.0)
    ends[0, 1, :, BLK:] = pack(points[:, own + BLK:own + 2 * BLK], zbuf[:, BLK:2 * BLK], two)
    pl.semaphore_wait(barrier, n_dev - 1)

    def halo_copy(turn, slot):
        shift = (1, 2, -1, -2)[slot]
        side = 0 if shift > 0 else 1
        target = me + shift
        return pltpu.make_async_remote_copy(
            src_ref=ends.at[turn, side], dst_ref=halo.at[turn, slot],
            send_sem=halo_send.at[turn, slot], recv_sem=halo_recv.at[turn, slot],
            device_id=(lax.rem(target + n_dev, n_dev),), device_id_type=pl.DeviceIdType.MESH)

    def sends(slot):
        shift = (1, 2, -1, -2)[slot]
        return (me + shift < n_dev) if shift > 0 else (me + shift >= 0)

    def receives(slot):
        shift = (1, 2, -1, -2)[slot]
        return (me - shift >= 0) if shift > 0 else (me - shift < n_dev)

    def halo_start(turn):
        for slot in range(4):
            @pl.when(sends(slot))
            def _():
                halo_copy(turn, slot).start()

    def halo_wait(turn):
        for slot in range(4):
            @pl.when(receives(slot))
            def _():
                halo_copy(turn, slot).wait_recv()
        for slot in range(4):
            @pl.when(sends(slot))
            def _():
                halo_copy(turn, slot).wait_send()

    halo_start(0)
    halo_wait(0)

    def ghosts(turn, rows):
        a = [halo[turn, s] for s in range(4)]
        left_two = halo[0, 0, 6:7, 0:BLK] > 0.5
        right_two = halo[0, 2, 6:7, BLK:] > 0.5
        l1 = a[0][:, BLK:]
        l0 = jnp.where(left_two, a[0][:, 0:BLK], a[1][:, BLK:])
        r0 = a[2][:, 0:BLK]
        r1 = jnp.where(right_two, a[2][:, BLK:], a[3][:, 0:BLK])
        parts = (l0, l1, r0, r1)
        return [jnp.concatenate([p[rows:rows + 3, :], jnp.zeros((5, BLK), F32)], axis=0) for p in parts]

    first = halo[0, 0]
    left1_live = first[6:7, BLK:] > 0.5
    left0_live = jnp.where(first[6:7, 0:BLK] > 0.5, first[6:7, 0:BLK], halo[0, 1, 6:7, BLK:]) > 0.5
    right0_live = halo[0, 2, 6:7, 0:BLK] > 0.5
    right1_live = jnp.where(halo[0, 2, 6:7, BLK:] > 0.5, halo[0, 2, 6:7, BLK:], halo[0, 3, 6:7, 0:BLK]) > 0.5
    left_two = first[6:7, 0:BLK] > 0.5
    right_two = halo[0, 2, 6:7, BLK:] > 0.5
    gp = ghosts(0, 0)
    gp[0] = jnp.where(left0_live, jnp.where(row8 == 0, gp[0] + jnp.where(left_two, 0.0, -0.5), gp[0]), FAR)
    gp[1] = jnp.where(left1_live, gp[1], FAR)
    gp[2] = jnp.where(right0_live, jnp.where(row8 == 0, gp[2] + countf * 0.5, gp[2]), FAR)
    gp[3] = jnp.where(right1_live, jnp.where(row8 == 0, gp[3] + (countf + jnp.where(right_two, 0.0, 1.0)) * 0.5, gp[3]), FAR)
    gz = ghosts(0, 3)

    wide_block = lax.broadcasted_iota(jnp.int32, (8, width + 2 * BLK), 1) >> 7
    at0 = wide_block == count
    at1 = wide_block == count + 1

    def extended(mid, tail, g):
        whole = jnp.concatenate([mid, tail], axis=1)
        whole = jnp.where(at0, jnp.concatenate([g[2]] * (nb + 2), axis=1), whole)
        whole = jnp.where(at1, jnp.concatenate([g[3]] * (nb + 2), axis=1), whole)
        return whole

    points[:, 0:BLK] = gp[0]
    points[:, BLK:2 * BLK] = gp[1]
    points[:, 2 * BLK:] = extended(points[:, 2 * BLK:2 * BLK + width], jnp.full((8, 2 * BLK), FAR, F32), gp)

    def turn_block(e, carry):
        at = pl.multiple_of(e * BLK, BLK)
        columns[pl.ds(at, BLK), :] = jnp.transpose(points[:, pl.ds(at, BLK)])
        return carry

    lax.fori_loop(0, nb + 4, turn_block, 0)

    def build_wing(b, carry):
        at = pl.multiple_of(b * BLK, BLK)
        here = points[:, pl.ds(pl.multiple_of(at + 2 * BLK, BLK), BLK)]
        build(kmat.at[b], columns, at, [here[c:c + 1, :] for c in range(3)])
        return carry

    lax.fori_loop(0, nb, build_wing, 0)

    def put_vector(turn, g):
        rows = slice(16 * turn, 16 * turn + 16)
        vext[rows, 0:BLK] = split(g[0])
        vext[rows, BLK:2 * BLK] = split(g[1])
        vext[rows, 2 * BLK:] = split(extended(zbuf[...], jnp.zeros((8, 2 * BLK), F32), g))

    def apply(turn):
        rows = slice(16 * turn, 16 * turn + 16)
        step = 4

        def group(q, carry):
            for u in range(step):
                b = q * step + u
                at = pl.multiple_of(b * BLK, BLK)
                o = jnp.dot(vext[rows, pl.ds(at, BAND * BLK)], kmat[b], preferred_element_type=F32)
                ibuf[:, pl.ds(at, BLK)] = o[0:8, 0:BLK] + o[8:16, 0:BLK] + o[0:8, BLK:]
            return carry

        lax.fori_loop(0, nb // step, group, 0)
        ibuf[...] = jnp.where(block_of < count, ibuf[...] + smooth_ref[...] * zbuf[...], 0.0)

    def lanes_sum(v):
        total = v[:, 0:BLK]
        for b in range(1, nb):
            total = total + v[:, b * BLK:(b + 1) * BLK]
        return jnp.sum(total, axis=1, keepdims=True)

    def sums_start(turn):
        norm = lanes_sum(rbuf[...] * zbuf[...])
        prod = lanes_sum(zbuf[...] * ibuf[...])
        spread = jnp.where(lane8 == row8, norm, 0.0) + jnp.where(lane8 == row8 + 8, prod, 0.0)
        sums[turn, me] = jnp.sum(spread, axis=0, keepdims=True)

        def send(k, carry):
            pltpu.make_async_remote_copy(
                src_ref=sums.at[turn, me], dst_ref=sums.at[turn, me],
                send_sem=sum_send.at[turn], recv_sem=sum_recv.at[turn],
                device_id=(lax.rem(me + k, n_dev),), device_id_type=pl.DeviceIdType.MESH).start()
            return carry

        lax.fori_loop(1, n_dev, send, 0)

    def sums_wait(turn):
        others = sums.at[turn, pl.ds(0, n_dev - 1)]
        pltpu.make_async_copy(others, others, sum_recv.at[turn]).wait()
        pltpu.make_async_copy(others, others, sum_send.at[turn]).wait()
        total = jnp.broadcast_to(jnp.sum(sums[turn], axis=0), (8, BLK))
        norm = jnp.sum(jnp.where(lane8 == row8, total, 0.0), axis=1, keepdims=True)
        prod = jnp.sum(jnp.where(lane8 == row8 + 8, total, 0.0), axis=1, keepdims=True)
        return norm, prod

    real = lax.broadcasted_iota(jnp.int32, (8, 1), 0) < 3

    def ratio(a, b):
        return jnp.where(real, a / jnp.where(real, b, 1.0), 0.0)

    ga = None
    norm_now = step_size = None
    gd = gc = None
    for turn in range(ITERS):
        put_vector(turn, gz)
        apply(turn)
        sums_start(turn)
        if turn + 1 < ITERS:
            wbuf[...] = ibuf[...] * inv[...]
            ends[turn + 1, 0, :, 0:BLK] = picked(wbuf, 0, count - 2)
            ends[turn + 1, 0, :, BLK:] = picked(wbuf, 0, count - 1)
            ends[turn + 1, 1, :, :] = wbuf[:, 0:2 * BLK]
            halo_start(turn + 1)
        norm_next, product = sums_wait(turn)
        if turn == 0:
            step_size = ratio(norm_next, product)
            dbuf[...] = zbuf[...]
            abuf[...] = ibuf[...]
            momentum = jnp.zeros((8, 1), F32)
            cbuf[...] = step_size * dbuf[...]
        else:
            momentum = ratio(norm_next, norm_now)
            step_size = ratio(norm_next, product - momentum * ratio(norm_next, step_size))
            dbuf[...] = zbuf[...] + momentum * dbuf[...]
            abuf[...] = ibuf[...] + momentum * abuf[...]
            cbuf[...] = cbuf[...] + step_size * dbuf[...]
        gd = gz if gd is None else [z + momentum * d for z, d in zip(gz, gd)]
        gc = [step_size * d for d in gd] if gc is None else [c + step_size * d for c, d in zip(gc, gd)]
        norm_now = norm_next
        rbuf[...] = rbuf[...] - step_size * abuf[...]
        if turn + 1 < ITERS:
            zbuf[...] = rbuf[...] * inv[...]
            halo_wait(turn + 1)
            gw = ghosts(turn + 1, 0)
            ga = gw if ga is None else [w + momentum * a for w, a in zip(gw, ga)]
            gz = [z - step_size * a for z, a in zip(gz, ga)]
    coef_out[...] = cbuf[0:3, :]
    resid_out[...] = rbuf[0:3, :]
    coef_ext[:, 0:BLK] = gc[0]
    coef_ext[:, BLK:2 * BLK] = gc[1]
    coef_ext[:, 2 * BLK:] = extended(cbuf[...], jnp.zeros((8, 2 * BLK), F32), gc)


def evaluator(nb, fb, live_ref, fluid_ref, points, coef_ext, fluid_out, columns, fpoints, vext, fmat, result):
    count = live_ref[0]
    fpoints[...] = jnp.zeros_like(fpoints)
    fpoints[0:3, :] = fluid_ref[...]
    vext[...] = split(coef_ext[...])

    def turn_block(e, carry):
        at = pl.multiple_of(e * BLK, BLK)
        columns[pl.ds(at, BLK), :] = jnp.transpose(points[:, pl.ds(at, BLK)])
        return carry

    lax.fori_loop(0, nb + 4, turn_block, 0)

    def block(f, slot):
        at = pl.multiple_of(f * BLK, BLK)
        anchor = lax.div(f * count, jnp.int32(fb))
        start = pl.multiple_of(anchor * BLK, BLK)
        here = fpoints[:, pl.ds(at, BLK)]
        row = [here[0:1, :] * 0.5 + anchor.astype(F32) * 0.5, here[1:2, :] * 3.0, here[2:3, :] * 3.0]
        build(fmat.at[slot], columns, start, row)
        o = jnp.dot(vext[:, pl.ds(start, BAND * BLK)], fmat[slot], preferred_element_type=F32)
        result[:, pl.ds(at, BLK)] = o[0:8, 0:BLK] + o[8:16, 0:BLK] + o[0:8, BLK:]

    def pair(q, carry):
        block(2 * q, 0)
        block(2 * q + 1, 1)
        return carry

    lax.fori_loop(0, fb // 2, pair, 0)
    fluid_out[...] = result[0:3, :]


def per_device(n_dev, wing_jitter, live_blocks, smoothing, displacement, fluid_jitter):
    width = wing_jitter.shape[1]
    fwidth = fluid_jitter.shape[1]
    nb = width // BLK
    fb = fwidth // BLK
    vmem = pl.BlockSpec(memory_space=pltpu.VMEM)
    wide = pltpu.VMEM((8, width), F32)
    ext = jax.ShapeDtypeStruct((8, width + 4 * BLK), F32)
    coefs, residual, points, coef_ext = pl.pallas_call(
        functools.partial(solver, n_dev, nb),
        name="solver",
        out_shape=(
            jax.ShapeDtypeStruct((3, width), F32),
            jax.ShapeDtypeStruct((3, width), F32),
            ext, ext,
        ),
        in_specs=[pl.BlockSpec(memory_space=pltpu.SMEM)] + [vmem] * 3,
        out_specs=(vmem,) * 4,
        scratch_shapes=[
            pltpu.VMEM((nb, BAND * BLK, 2 * BLK), BF16),
            pltpu.VMEM((width + 4 * BLK, 8), F32),
            pltpu.VMEM((ITERS, 2, 8, 2 * BLK), F32),
            pltpu.VMEM((ITERS, 4, 8, 2 * BLK), F32),
            pltpu.VMEM((ITERS, n_dev, 1, BLK), F32),
            pltpu.VMEM((16 * ITERS, width + 4 * BLK), BF16),
            wide, wide, wide, wide, wide, wide, wide, wide,
            pltpu.SemaphoreType.DMA((ITERS, 4)),
            pltpu.SemaphoreType.DMA((ITERS, 4)),
            pltpu.SemaphoreType.DMA((ITERS,)),
            pltpu.SemaphoreType.DMA((ITERS,)),
        ],
        compiler_params=pltpu.CompilerParams(
            collective_id=0, has_side_effects=True, vmem_limit_bytes=48 * 1024 * 1024),
    )(live_blocks, wing_jitter, smoothing.reshape(1, width), displacement)
    fluid_values = pl.pallas_call(
        functools.partial(evaluator, nb, fb),
        name="evaluator",
        out_shape=jax.ShapeDtypeStruct((3, fwidth), F32),
        in_specs=[pl.BlockSpec(memory_space=pltpu.SMEM)] + [vmem] * 3,
        out_specs=vmem,
        scratch_shapes=[
            pltpu.VMEM((width + 4 * BLK, 8), F32),
            pltpu.VMEM((8, fwidth), F32),
            pltpu.VMEM((16, width + 4 * BLK), BF16),
            pltpu.VMEM((2, BAND * BLK, 2 * BLK), BF16),
            pltpu.VMEM((8, fwidth), F32),
        ],
        compiler_params=pltpu.CompilerParams(vmem_limit_bytes=16 * 1024 * 1024),
    )(live_blocks, fluid_jitter, points, coef_ext)
    return coefs, residual, fluid_values


def solution(mesh):
    return jax.shard_map(
        functools.partial(per_device, mesh.shape["dom"]),
        mesh=mesh,
        in_specs=(P(None, "dom"), P("dom"), P("dom"), P(None, "dom"), P(None, "dom")),
        out_specs=(P(None, "dom"), P(None, "dom"), P(None, "dom")),
        check_vma=False,
    )
```

time: 646 us -> 95.3 us (0.15)
  matrix products: 157 us -> 0 us
  blocking collectives: 134 us -> 0 us
  loops' own time: 133 us -> 0 us
  local copies, waits for them, and re-layouts: 131 us -> 3.87 us
  Pallas kernels: 0 us -> 89.9 us
  starting transfers between devices: 56.2 us -> 0 us
  waiting for transfers between devices: 15.1 us -> 0 us
  other arithmetic: 8.18 us -> 0 us
    dot_general x120 -> x0, matrix products: 157 us -> none  [the longest x96 126 us: row_group(): jnp.einsum('cj,ij->ci', col_values, kernel, precision=lax.Precision.HIGHEST)]
    psum x3 -> x0, blocking collectives: 134 us -> none  [two_products(): lax.psum((jnp.sum(residual * precond, axis=1), jnp.sum(precond * image, a...]
    another operation x4 -> x0, loops' own time: 133 us -> none  [the longest x1 66.8 us: per_device(): lax.map(fluid_block, jnp.arange(fluid_count, dtype=jnp.int32))]
    dynamic_slice x264 -> x0, local copies, waits for them, and re-layouts: 101 us -> none  [the longest x96 59.9 us: apply(): result = lax.map(row_group, jnp.arange(block_count // 2, dtype=jnp.int32))]
    pallas_call x0 -> x2, Pallas kernels: none -> 89.9 us  [the longest x1 71.2 us: per_device(): pl.pallas_call(functools.partial(solver, n_dev, nb), name='solver', out_s...]
    ppermute x24 -> x0, starting transfers between devices: 56.2 us -> none  [from_behind(): return lax.ppermute(block, axis, route)]
    slice x220 -> x0, local copies, waits for them, and re-layouts: 22.3 us -> none  [the longest x216 20 us: wendland(): spread = (row_points[0][:, None] - col_points[0][None, :]) ** 2]
    ppermute x24 -> x0, waiting for transfers between devices: 15.1 us -> none  [from_behind(): return lax.ppermute(block, axis, route)]
  transfers between devices with their start and end apart: 24 -> 0, of which waited for: 8 -> 0; matrix products, arithmetic and copies ran while one was open for 3% -> 0% of each run, Pallas kernels for 0% -> 0%
where the time goes in v1:
time: 95.3 us; the launch traced here: 95.1 us
  Pallas kernels  89.9 us (94%)
  local copies, waits for them, and re-layouts  3.87 us (4%)
  between operations  1.3 us (1%)
    pallas_call x1, Pallas kernels, per_device(): pl.pallas_call(functools.partial(solver, n_dev, nb), name='solver', out_s...  71.2 us
    pallas_call x1, Pallas kernels, per_device(): pl.pallas_call(functools.partial(evaluator, nb, fb), name='evaluator', ou...  18.7 us
    unnamed x10, local copies, waits for them, and re-layouts  3.87 us

profile of v1, /device:TPU:0, one launch (start us, length us, event | category | flops | bytes accessed | tf_op | source)
XLA Modules:
  0.0 95.1 jit_solution(17800809302185728608)
XLA Ops:
  1.3 0.0 copy-start
  1.3 0.9 copy-done
  2.2 0.0 copy-start.1
  2.2 0.9 copy-done.1
  3.1 0.0 copy-start.3
  3.1 0.8 copy-done.3
  3.8 0.0 copy-start.2
  3.8 71.2 %solver.1 = (f32[3,8192]{1,0:T(4,128)S(1)}, f32[3,8192]{1,0:T(4,128)S(1)}, f32[8,8704]{1,0:T(8,128)S(1)}, f32[8,8704]{1,0:T(8,128)S(1)}) custom-call(s32[1]{0:T(128)S(6)} %copy.10.live_ref, f32[3,8192]{1,0:T(4,128)S(1)} %copy-done, f32[1,8192]{1,0:T(1,128)S(1)} %bitcast.1, f32[3,8192]{1,0:T(4,128)S(1)} %copy-done.1), custom_call_target="tpu_custom_call" | custom-call | tf_op jit(solution)/shard_map/solver/pallas_call | solution.py:334
  75.0 0.0 copy-done.2
  75.1 18.7 %evaluator.1 = f32[3,3072]{1,0:T(4,128)} custom-call(s32[1]{0:T(128)S(6)} %copy.10.live_ref, f32[3,3072]{1,0:T(4,128)S(1)} %copy-done.2, f32[8,8704]{1,0:T(8,128)S(1)} %get-tuple-element.9.points, f32[8,8704]{1,0:T(8,128)S(1)} %get-tuple-element.10.coef_ext), custom_call_target="tpu_custom_call" | custom-call | tf_op jit(solution)/shard_map/evaluator/pallas_call | solution.py:360
  93.8 0.7 copy.11
  94.4 0.7 copy.12
Async XLA Ops:
  1.3 0.9 copy-start
  2.2 0.9 copy-start.1
  3.1 0.8 copy-start.3
  3.8 71.2 %copy-start.2 = (f32[3,3072]{1,0:T(4,128)S(1)}, f32[3,3072]{1,0:T(4,128)}, u32[]{:S(2)}) copy-start(f32[3,3072]{1,0:T(4,128)} %fluid_ref.1) | copy-start | bytes 110596

commit v2 on v1

--- a/solution.py
+++ b/solution.py
@@ -10,27 +10,63 @@
 BLK = 128
 ITERS = 3
 BAND = 5
-FAR = 1.0e4
+FAR = 64.0
+FEATURES = 48
 F32 = jnp.float32
 BF16 = jnp.bfloat16
 
 
-def phi_of(row, col):
-    dx = row[0] - col[0]
-    dy = row[1] - col[1]
-    dz = row[2] - col[2]
-    spread = jnp.maximum(dx * dx + dy * dy + dz * dz, 1e-30)
+def phi_of(spread):
+    spread = jnp.maximum(spread, 1e-30)
     scaled = spread * lax.rsqrt(spread)
     remain = jnp.maximum(1.0 - scaled, 0.0)
     square = remain * remain
     return square * square * (5.0 - 4.0 * remain)
 
 
-def build(dest, columns, first_col, row):
+def row_ids(width):
+    return lax.broadcasted_iota(jnp.int32, (8, width), 0)
+
+
+def three_terms(v):
+    high = v.astype(BF16).astype(F32)
+    rest = v - high
+    mid = rest.astype(BF16).astype(F32)
+    return high, mid, rest - mid
+
+
+def column_features(p):
+    rows = row_ids(BLK)
+    norm = jnp.sum(p * p, axis=0, keepdims=True)
+    high, mid, low = three_terms(jnp.where(rows == 3, norm, jnp.where(rows == 4, 1.0, p)))
+    return jnp.concatenate([high, high, mid, high, low, mid], axis=0)
+
+
+def row_features(p, shift):
+    rows = row_ids(BLK)
+    q = jnp.where(rows == 0, p - shift, p)
+    norm = jnp.sum(q * q, axis=0, keepdims=True)
+    high, mid, low = three_terms(jnp.where(rows == 3, 1.0, jnp.where(rows == 4, norm, -2.0 * q)))
+    return jnp.concatenate([high, mid, high, low, high, mid], axis=0).astype(BF16)
+
+
+def turn_columns(points, columns, blocks):
+    def turn_block(q, carry):
+        for u in range(2):
+            at = pl.multiple_of((2 * q + u) * BLK, BLK)
+            features = column_features(points[:, pl.ds(at, BLK)])
+            columns[pl.ds(at, BLK), :] = jnp.transpose(features).astype(BF16)
+        return carry
+
+    lax.fori_loop(0, blocks // 2, turn_block, 0)
+
+
+def build(dest, columns, first_col, here):
     for delta in range(BAND):
         at = pl.multiple_of(first_col + delta * BLK, BLK)
-        cols = columns[pl.ds(at, BLK), :]
-        value = phi_of([cols[:, c:c + 1] for c in range(3)], row)
+        spread = jnp.dot(columns[pl.ds(at, BLK), :], row_features(here, (delta - BAND // 2) * 0.5),
+                         preferred_element_type=F32)
+        value = phi_of(spread)
         high = value.astype(BF16)
         low = (value - high.astype(F32)).astype(BF16)
         dest[delta * BLK:(delta + 1) * BLK, 0:BLK] = high
@@ -61,13 +97,12 @@
 
     block_of = lax.broadcasted_iota(jnp.int32, (8, width), 1) >> 7
     live = block_of < count
-    along_x = block_of.astype(F32)
     row_id = lax.broadcasted_iota(jnp.int32, (8, width), 0)
     zbuf[...] = jnp.zeros_like(zbuf)
     zbuf[0:3, :] = wing_ref[...]
     scale = jnp.where(row_id == 0, 0.5, 3.0)
-    pts = zbuf[...] * scale + jnp.where(row_id == 0, along_x * 0.5, 0.0)
-    pts = jnp.where(live, pts, FAR)
+    pts = zbuf[...] * scale - jnp.where(row_id == 0, 0.0, 1.5)
+    pts = jnp.where(row_id < 3, jnp.where(live, pts, FAR), 0.0)
     points[:, 2 * BLK:2 * BLK + width] = pts
     smooth = jnp.broadcast_to(smooth_ref[...], (8, width))
     inv[...] = 1.0 / (1.0 + smooth)
@@ -87,17 +122,13 @@
 
     two = (count >= 2).astype(F32)
 
-    def shifted(p, base):
-        return jnp.where(row8 == 0, p - base * 0.5, p)
-
     def pack(p, z, flag):
         low = jnp.concatenate([p[0:3, :], z[0:3, :], jnp.full((2, BLK), 1.0, F32) * flag], axis=0)
         return low
 
-    countf = count.astype(F32)
     own = 2 * BLK
-    ends[0, 0, :, 0:BLK] = pack(shifted(picked(points, own, count - 2), countf), picked(zbuf, 0, count - 2), two)
-    ends[0, 0, :, BLK:] = pack(shifted(picked(points, own, count - 1), countf), picked(zbuf, 0, count - 1), 1.0)
+    ends[0, 0, :, 0:BLK] = pack(picked(points, own, count - 2), picked(zbuf, 0, count - 2), two)
+    ends[0, 0, :, BLK:] = pack(picked(points, own, count - 1), picked(zbuf, 0, count - 1), 1.0)
     ends[0, 1, :, 0:BLK] = pack(points[:, own:own + BLK], zbuf[:, 0:BLK], 1.0)
     ends[0, 1, :, BLK:] = pack(points[:, own + BLK:own + 2 * BLK], zbuf[:, BLK:2 * BLK], two)
     pl.semaphore_wait(barrier, n_dev - 1)
@@ -154,13 +185,9 @@
     left0_live = jnp.where(first[6:7, 0:BLK] > 0.5, first[6:7, 0:BLK], halo[0, 1, 6:7, BLK:]) > 0.5
     right0_live = halo[0, 2, 6:7, 0:BLK] > 0.5
     right1_live = jnp.where(halo[0, 2, 6:7, BLK:] > 0.5, halo[0, 2, 6:7, BLK:], halo[0, 3, 6:7, 0:BLK]) > 0.5
-    left_two = first[6:7, 0:BLK] > 0.5
-    right_two = halo[0, 2, 6:7, BLK:] > 0.5
     gp = ghosts(0, 0)
-    gp[0] = jnp.where(left0_live, jnp.where(row8 == 0, gp[0] + jnp.where(left_two, 0.0, -0.5), gp[0]), FAR)
-    gp[1] = jnp.where(left1_live, gp[1], FAR)
-    gp[2] = jnp.where(right0_live, jnp.where(row8 == 0, gp[2] + countf * 0.5, gp[2]), FAR)
-    gp[3] = jnp.where(right1_live, jnp.where(row8 == 0, gp[3] + (countf + jnp.where(right_two, 0.0, 1.0)) * 0.5, gp[3]), FAR)
+    away = jnp.where(row8 < 3, FAR, 0.0)
+    gp = [jnp.where(seen, g, away) for seen, g in zip((left0_live, left1_live, right0_live, right1_live), gp)]
     gz = ghosts(0, 3)
 
     wide_block = lax.broadcasted_iota(jnp.int32, (8, width + 2 * BLK), 1) >> 7
@@ -175,22 +202,18 @@
 
     points[:, 0:BLK] = gp[0]
     points[:, BLK:2 * BLK] = gp[1]
-    points[:, 2 * BLK:] = extended(points[:, 2 * BLK:2 * BLK + width], jnp.full((8, 2 * BLK), FAR, F32), gp)
-
-    def turn_block(e, carry):
-        at = pl.multiple_of(e * BLK, BLK)
-        columns[pl.ds(at, BLK), :] = jnp.transpose(points[:, pl.ds(at, BLK)])
+    points[:, 2 * BLK:] = extended(points[:, 2 * BLK:2 * BLK + width], jnp.concatenate([away, away], axis=1), gp)
+
+    turn_columns(points, columns, nb + 4)
+
+    def build_wing(q, carry):
+        for u in range(2):
+            b = 2 * q + u
+            at = pl.multiple_of(b * BLK, BLK)
+            build(kmat.at[b], columns, at, points[:, pl.ds(pl.multiple_of(at + 2 * BLK, BLK), BLK)])
         return carry
 
-    lax.fori_loop(0, nb + 4, turn_block, 0)
-
-    def build_wing(b, carry):
-        at = pl.multiple_of(b * BLK, BLK)
-        here = points[:, pl.ds(pl.multiple_of(at + 2 * BLK, BLK), BLK)]
-        build(kmat.at[b], columns, at, [here[c:c + 1, :] for c in range(3)])
-        return carry
-
-    lax.fori_loop(0, nb, build_wing, 0)
+    lax.fori_loop(0, nb // 2, build_wing, 0)
 
     def put_vector(turn, g):
         rows = slice(16 * turn, 16 * turn + 16)
@@ -295,22 +318,18 @@
     count = live_ref[0]
     fpoints[...] = jnp.zeros_like(fpoints)
     fpoints[0:3, :] = fluid_ref[...]
+    rows = row_ids(fpoints.shape[1])
+    fpoints[...] = fpoints[...] * jnp.where(rows == 0, 0.5, 3.0) - jnp.where((rows == 1) | (rows == 2), 1.5, 0.0)
     vext[...] = split(coef_ext[...])
 
-    def turn_block(e, carry):
-        at = pl.multiple_of(e * BLK, BLK)
-        columns[pl.ds(at, BLK), :] = jnp.transpose(points[:, pl.ds(at, BLK)])
-        return carry
-
-    lax.fori_loop(0, nb + 4, turn_block, 0)
+    turn_columns(points, columns, nb + 4)
 
     def block(f, slot):
         at = pl.multiple_of(f * BLK, BLK)
         anchor = lax.div(f * count, jnp.int32(fb))
         start = pl.multiple_of(anchor * BLK, BLK)
         here = fpoints[:, pl.ds(at, BLK)]
-        row = [here[0:1, :] * 0.5 + anchor.astype(F32) * 0.5, here[1:2, :] * 3.0, here[2:3, :] * 3.0]
-        build(fmat.at[slot], columns, start, row)
+        build(fmat.at[slot], columns, start, here)
         o = jnp.dot(vext[:, pl.ds(start, BAND * BLK)], fmat[slot], preferred_element_type=F32)
         result[:, pl.ds(at, BLK)] = o[0:8, 0:BLK] + o[8:16, 0:BLK] + o[0:8, BLK:]
 
@@ -343,7 +362,7 @@
         out_specs=(vmem,) * 4,
         scratch_shapes=[
             pltpu.VMEM((nb, BAND * BLK, 2 * BLK), BF16),
-            pltpu.VMEM((width + 4 * BLK, 8), F32),
+            pltpu.VMEM((width + 4 * BLK, FEATURES), BF16),
             pltpu.VMEM((ITERS, 2, 8, 2 * BLK), F32),
             pltpu.VMEM((ITERS, 4, 8, 2 * BLK), F32),
             pltpu.VMEM((ITERS, n_dev, 1, BLK), F32),
@@ -364,7 +383,7 @@
         in_specs=[pl.BlockSpec(memory_space=pltpu.SMEM)] + [vmem] * 3,
         out_specs=vmem,
         scratch_shapes=[
-            pltpu.VMEM((width + 4 * BLK, 8), F32),
+            pltpu.VMEM((width + 4 * BLK, FEATURES), BF16),
             pltpu.VMEM((8, fwidth), F32),
             pltpu.VMEM((16, width + 4 * BLK), BF16),
             pltpu.VMEM((2, BAND * BLK, 2 * BLK), BF16),

time: 95.3 us -> 78.2 us (0.82)
  Pallas kernels: 89.9 us -> 72.8 us
    pallas_call x1, Pallas kernels: 71.2 us -> 58.5 us  [per_device(): pl.pallas_call(functools.partial(solver, n_dev, nb), name='solver', out_s...]
    pallas_call x1, Pallas kernels: 18.7 us -> 14.4 us  [per_device(): pl.pallas_call(functools.partial(evaluator, nb, fb), name='evaluator', ou...]
where the time goes in v2:
time: 78.2 us; the launch traced here: 78 us
  Pallas kernels  72.8 us (93%)
  local copies, waits for them, and re-layouts  3.87 us (5%)
  between operations  1.3 us (2%)
    pallas_call x1, Pallas kernels, per_device(): pl.pallas_call(functools.partial(solver, n_dev, nb), name='solver', out_s...  58.5 us
    pallas_call x1, Pallas kernels, per_device(): pl.pallas_call(functools.partial(evaluator, nb, fb), name='evaluator', ou...  14.4 us
    unnamed x10, local copies, waits for them, and re-layouts  3.87 us

profile of v2, /device:TPU:0, one launch (start us, length us, event | category | flops | bytes accessed | tf_op | source)
XLA Modules:
  0.0 78.0 jit_solution(8280811631972508065)
XLA Ops:
  1.3 0.0 copy-start
  1.3 0.9 %copy-done = f32[3,8192]{1,0:T(4,128)S(1)} copy-done((f32[3,8192]{1,0:T(4,128)S(1)}, f32[3,8192]{1,0:T(4,128)}, u32[]{:S(2)}) %copy-start) | copy-done | bytes 98328
  2.2 0.0 copy-start.1
  2.2 0.9 %copy-done.1 = f32[3,8192]{1,0:T(4,128)S(1)} copy-done((f32[3,8192]{1,0:T(4,128)S(1)}, f32[3,8192]{1,0:T(4,128)}, u32[]{:S(2)}) %copy-start.1) | copy-done | bytes 98328
  3.1 0.0 copy-start.3
  3.1 0.8 copy-done.3
  3.8 0.0 copy-start.2
  3.8 58.5 %solver.1 = (f32[3,8192]{1,0:T(4,128)S(1)}, f32[3,8192]{1,0:T(4,128)S(1)}, f32[8,8704]{1,0:T(8,128)S(1)}, f32[8,8704]{1,0:T(8,128)S(1)}) custom-call(s32[1]{0:T(128)S(6)} %copy.10.live_ref, f32[3,8192]{1,0:T(4,128)S(1)} %copy-done, f32[1,8192]{1,0:T(1,128)S(1)} %bitcast.1, f32[3,8192]{1,0:T(4,128)S(1)} %copy-done.1), custom_call_target="tpu_custom_call" | custom-call | tf_op jit(solution)/shard_map/solver/pallas_call | solution.py:353
  62.3 0.0 copy-done.2
  62.3 14.4 %evaluator.1 = f32[3,3072]{1,0:T(4,128)} custom-call(s32[1]{0:T(128)S(6)} %copy.10.live_ref, f32[3,3072]{1,0:T(4,128)S(1)} %copy-done.2, f32[8,8704]{1,0:T(8,128)S(1)} %get-tuple-element.9.points, f32[8,8704]{1,0:T(8,128)S(1)} %get-tuple-element.10.coef_ext), custom_call_target="tpu_custom_call" | custom-call | tf_op jit(solution)/shard_map/evaluator/pallas_call | solution.py:379
  76.7 0.7 copy.11
  77.3 0.7 copy.12
Async XLA Ops:
  1.3 0.9 %copy-start = (f32[3,8192]{1,0:T(4,128)S(1)}, f32[3,8192]{1,0:T(4,128)}, u32[]{:S(2)}) copy-start(f32[3,8192]{1,0:T(4,128)} %wing_ref.1) | copy-start | bytes 294916
  2.2 0.9 %copy-start.1 = (f32[3,8192]{1,0:T(4,128)S(1)}, f32[3,8192]{1,0:T(4,128)}, u32[]{:S(2)}) copy-start(f32[3,8192]{1,0:T(4,128)} %disp_ref.1) | copy-start | bytes 294916
  3.1 0.8 copy-start.3
  3.8 58.5 %copy-start.2 = (f32[3,3072]{1,0:T(4,128)S(1)}, f32[3,3072]{1,0:T(4,128)}, u32[]{:S(2)}) copy-start(f32[3,3072]{1,0:T(4,128)} %fluid_ref.1) | copy-start | bytes 110596
